TPU v7x, 32 devices: a whole 2x2x4 slice. The times are simulated.
32 devices in a mesh: expert: 4 (over y, core), fsdp: 8 (over z, x).
Axes of the slice: x: 2, y: 2, z: 4, core: 2. Of those that a mesh axis runs over, the one named last changes fastest.
Arguments:
- gradients: bfloat16 [8, 3584, 1024], P('expert', 'fsdp'), may hold values from -24 to 24, as said below
- owner: int32 [4, 2], P('expert'), may hold values from 0 to 1, each once within a row
Outputs:
- updates: bfloat16 [8, 3584, 1024], P('expert', 'fsdp')
- slot_rms: float32 [4, 8], P('expert', 'fsdp')
Inputs may be any that keep to these rules, and one draw needn't show every extreme that they name: gradients are values of mean zero and unit variance times a factor per expert between 0.5 and 2 and a factor per expert and row slice between 0.5 and 2, each entry within 24 in magnitude. Each row of owner names every place 0 to 1 exactly once.
All inputs are finite; a program needn't handle non-finite values.
Results may differ from a plain program's by a relative error of at most 0.009.
Values may be sent and summed in bfloat16 or wider, within the bound.
A program may use at most 64 MiB of HBM per device.

v0:
```python
import math
import jax
import jax.numpy as jnp
from jax import lax
from jax.sharding import PartitionSpec as P

ROWS = 3584
COLS = 1024
SHARE = 4
ITERS = 3
coef_a = 3.4445
coef_b = -4.775
coef_c = 2.0315
epsilon = 1e-07


def as_sent(value):
    return jax.tree.map(lambda a: a.astype(jnp.bfloat16) if a.dtype == jnp.float32 else a, value)


def partner_2(value, axis, distance):
    mask = 2**distance
    pairs = [(source, source ^ mask) for source in range(lax.axis_size(axis))]
    return lax.ppermute(value, axis, pairs)


def select_half(stacked, bit_value):
    retained = lax.dynamic_index_in_dim(stacked, bit_value, 0, keepdims=False)
    outgoing = lax.dynamic_index_in_dim(stacked, 1 - bit_value, 0, keepdims=False)
    return (retained, outgoing)


def join_halves(own_block, theirs, bit_value):
    leading = jnp.where(bit_value == 0, own_block, theirs)
    trailing = jnp.where(bit_value == 0, theirs, own_block)
    return jnp.concatenate([leading, trailing], axis=0)


def reduce_gram(current, low_bit, high_bit):
    partial_gram = lax.dot_general(
        current, current, (((0,), (0,)), ((), ())), preferred_element_type=jnp.float32
    )
    rounded = lax.optimization_barrier(partial_gram.astype(jnp.bfloat16))
    columns = rounded.shape[1]
    retained, outgoing = select_half(rounded.reshape(2, columns // 2, columns), low_bit)
    arrived = partner_2(as_sent(outgoing), "fsdp", 0).astype(outgoing.dtype)
    pair_sum = retained.astype(jnp.float32) + arrived.astype(jnp.float32)
    retained_pair, outgoing_pair = select_half(pair_sum.reshape(2, columns // 4, columns), high_bit)
    arrived_pair = partner_2(as_sent(outgoing_pair), "fsdp", 1).astype(outgoing_pair.dtype)
    return (retained_pair + arrived_pair).astype(jnp.bfloat16)


def spread_gram(quarter, low_bit, high_bit):
    incoming = partner_2(quarter, "fsdp", 1)
    half_block = join_halves(quarter, incoming, high_bit)
    partner = partner_2(as_sent(half_block), "fsdp", 0).astype(half_block.dtype)
    return join_halves(half_block, partner, low_bit)


def body(gradients, owner):
    expert_count, local_rows, columns = gradients.shape
    fsdp_index = lax.axis_index("fsdp")
    low_bit = fsdp_index % 2
    high_bit = fsdp_index // 2 % 2
    owner_row = owner[0]
    places = jnp.arange(expert_count, dtype=jnp.int32)
    inverse = jnp.sum(
        jnp.where(owner_row[None, :] == places[:, None], places[None, :], 0), axis=1
    ).astype(jnp.int32)
    expert_sums = jnp.sum(jnp.square(gradients.astype(jnp.float32)), axis=(1, 2))
    totals = lax.psum(expert_sums, "fsdp")
    own_expert = lax.dynamic_index_in_dim(inverse, fsdp_index // SHARE, 0, keepdims=False)
    square_sum = lax.dynamic_index_in_dim(totals, own_expert, 0, keepdims=False)
    ordered = jnp.take(gradients, inverse, axis=0)
    outbound = ordered.reshape(expert_count * SHARE, local_rows // SHARE, columns)
    held = lax.all_to_all(outbound, "fsdp", split_axis=0, concat_axis=1, tiled=True)[0]
    norm_value = jnp.sqrt(square_sum)
    current = (held.astype(jnp.float32) / (norm_value + epsilon)).astype(jnp.bfloat16)
    for iteration in range(ITERS):
        quarter = reduce_gram(current, low_bit, high_bit)
        gram_full = spread_gram(quarter, low_bit, high_bit)
        squared = jnp.dot(gram_full, gram_full, preferred_element_type=jnp.float32)
        poly = (coef_b * gram_full.astype(jnp.float32) + coef_c * squared).astype(jnp.bfloat16)
        current = (
            coef_a * current.astype(jnp.float32)
            + jnp.dot(current, poly, preferred_element_type=jnp.float32)
        ).astype(jnp.bfloat16)
    update = (math.sqrt(ROWS) * current.astype(jnp.float32)).astype(jnp.bfloat16)
    returned = lax.all_to_all(update[None], "fsdp", split_axis=1, concat_axis=0, tiled=True)
    slot_order = returned.reshape(expert_count, local_rows, columns)
    updates = jnp.take(slot_order, owner_row, axis=0)
    slot_rms = (norm_value / math.sqrt(ROWS * COLS)).reshape(1, 1).astype(jnp.float32)
    return (updates, slot_rms)


def solution(mesh):
    placed = (P("expert", "fsdp", None), P("expert", None))
    return jax.shard_map(
        body,
        mesh=mesh,
        in_specs=placed,
        out_specs=(P("expert", "fsdp", None), P("expert", "fsdp")),
        check_vma=False,
    )
```

profile of v0, /device:TPU:0, one launch (start us, length us, event | category | flops | bytes accessed | tf_op | source)
XLA Modules:
  0.0 340.0 jit_solution(16962302694401268506)
XLA Ops:
  2.7 2.2 gather_fusion
  6.4 7.3 %all-to-all-start = ((bf16[8,112,1024]{2,1,0:T(8,128)(2,1)}), bf16[8,112,1024]{2,1,0:T(8,128)(2,1)S(1)}, u32[]{:S(2)}, u32[]{:S(2)}) async-start(bf16[8,112,1024]{2,1,0:T(8,128)(2,1)} %bitcast.71), calls=%async_computation | async-start | bytes 3670016 | tf_op jit(solution)/shard_map/all_to_all | solution.py:76
  15.7 43.7 %psum.7 = f32[2]{0:T(128)S(1)} all-reduce(f32[2]{0:T(128)S(1)} %multiply_reduce_fusion), channel_id=1, replica_groups=mesh['expert'=4,'fsdp'=8] {'fsdp'}, use_global_device_ids=true, to_apply=%region_2.4 | all-reduce | flops 2 | bytes 16 | tf_op jit(solution)/shard_map/psum | solution.py:71
  63.7 2.4 bitcast_convert_fusion
  67.5 5.0 %collective-permute-start = (bf16[512,1024]{1,0:T(8,128)(2,1)S(1)}, bf16[512,1024]{1,0:T(8,128)(2,1)S(1)}, u32[]{:S(2)}, u32[]{:S(2)}) collective-permute-start(bf16[512,1024]{1,0:T(8,128)(2,1)S(1)} %dynamic-slice_bitcast_fusion.2), channel_id=1, source_target_pairs={{0,1},{1,0},{2,3},{3,2},{4,5},{5,4},{6,7},{7,6},{8,9},{9,8},{10,11... | collective-permute-start | bytes 3145736 | tf_op jit(solution)/shard_map/ppermute | solution.py:24
  72.6 19.5 %collective-permute-done = bf16[512,1024]{1,0:T(8,128)(2,1)S(1)} collective-permute-done((bf16[512,1024]{1,0:T(8,128)(2,1)S(1)}, bf16[512,1024]{1,0:T(8,128)(2,1)S(1)}, u32[]{:S(2)}, u32[]{:S(2)}) %collective-permute-start) | collective-permute-done | bytes 1048608 | tf_op jit(solution)/shard_map/ppermute | solution.py:24
  93.7 3.4 collective-permute-start.1
  97.1 9.9 %collective-permute-done.1 = bf16[256,1024]{1,0:T(8,128)(2,1)S(1)} collective-permute-done((bf16[256,1024]{1,0:T(8,128)(2,1)S(1)}, bf16[256,1024]{1,0:T(8,128)(2,1)S(1)}, u32[]{:S(2)}, u32[]{:S(2)}) %collective-permute-start.1) | collective-permute-done | bytes 524320 | tf_op jit(solution)/shard_map/ppermute | solution.py:24
  109.2 7.2 %collective-permute-done.2 = bf16[256,1024]{1,0:T(8,128)(2,1)S(1)} collective-permute-done((bf16[256,1024]{1,0:T(8,128)(2,1)S(1)}, bf16[256,1024]{1,0:T(8,128)(2,1)S(1)}, u32[]{:S(2)}, u32[]{:S(2)}) %collective-permute-start.2) | collective-permute-done | bytes 524320 | tf_op jit(solution)/shard_map/ppermute | solution.py:24
  116.5 2.2 collective-permute-start.3
  118.7 18.2 %collective-permute-done.3 = bf16[512,1024]{1,0:T(8,128)(2,1)S(1)} collective-permute-done((bf16[512,1024]{1,0:T(8,128)(2,1)S(1)}, bf16[512,1024]{1,0:T(8,128)(2,1)S(1)}, u32[]{:S(2)}, u32[]{:S(2)}) %collective-permute-start.3) | collective-permute-done | bytes 1048608 | tf_op jit(solution)/shard_map/ppermute | solution.py:24
  137.4 2.5 add_convert_fusion.2
  141.9 2.4 convolution_convert_fusion.1
  146.2 17.6 %collective-permute-done.4 = bf16[512,1024]{1,0:T(8,128)(2,1)S(1)} collective-permute-done((bf16[512,1024]{1,0:T(8,128)(2,1)S(1)}, bf16[512,1024]{1,0:T(8,128)(2,1)S(1)}, u32[]{:S(2)}, u32[]{:S(2)}) %collective-permute-start.4) | collective-permute-done | bytes 1048608 | tf_op jit(solution)/shard_map/ppermute | solution.py:24
  165.3 13.1 %collective-permute-done.5 = bf16[256,1024]{1,0:T(8,128)(2,1)S(1)} collective-permute-done((bf16[256,1024]{1,0:T(8,128)(2,1)S(1)}, bf16[256,1024]{1,0:T(8,128)(2,1)S(1)}, u32[]{:S(2)}, u32[]{:S(2)}) %collective-permute-start.5) | collective-permute-done | bytes 524320 | tf_op jit(solution)/shard_map/ppermute | solution.py:24
  180.1 7.7 %collective-permute-done.6 = bf16[256,1024]{1,0:T(8,128)(2,1)S(1)} collective-permute-done((bf16[256,1024]{1,0:T(8,128)(2,1)S(1)}, bf16[256,1024]{1,0:T(8,128)(2,1)S(1)}, u32[]{:S(2)}, u32[]{:S(2)}) %collective-permute-start.6) | collective-permute-done | bytes 524320 | tf_op jit(solution)/shard_map/ppermute | solution.py:24
  189.8 14.4 %collective-permute-done.7 = bf16[512,1024]{1,0:T(8,128)(2,1)S(1)} collective-permute-done((bf16[512,1024]{1,0:T(8,128)(2,1)S(1)}, bf16[512,1024]{1,0:T(8,128)(2,1)S(1)}, u32[]{:S(2)}, u32[]{:S(2)}) %collective-permute-start.7) | collective-permute-done | bytes 1048608 | tf_op jit(solution)/shard_map/ppermute | solution.py:24
  204.9 2.7 add_convert_fusion.1
  209.6 2.4 convolution_convert_fusion
  213.7 13.9 %collective-permute-done.8 = bf16[512,1024]{1,0:T(8,128)(2,1)S(1)} collective-permute-done((bf16[512,1024]{1,0:T(8,128)(2,1)S(1)}, bf16[512,1024]{1,0:T(8,128)(2,1)S(1)}, u32[]{:S(2)}, u32[]{:S(2)}) %collective-permute-start.8) | collective-permute-done | bytes 1048608 | tf_op jit(solution)/shard_map/ppermute | solution.py:24
  228.7 11.2 %collective-permute-done.9 = bf16[256,1024]{1,0:T(8,128)(2,1)S(1)} collective-permute-done((bf16[256,1024]{1,0:T(8,128)(2,1)S(1)}, bf16[256,1024]{1,0:T(8,128)(2,1)S(1)}, u32[]{:S(2)}, u32[]{:S(2)}) %collective-permute-start.9) | collective-permute-done | bytes 524320 | tf_op jit(solution)/shard_map/ppermute | solution.py:24
  240.4 8.9 %collective-permute-done.10 = bf16[256,1024]{1,0:T(8,128)(2,1)S(1)} collective-permute-done((bf16[256,1024]{1,0:T(8,128)(2,1)S(1)}, bf16[256,1024]{1,0:T(8,128)(2,1)S(1)}, u32[]{:S(2)}, u32[]{:S(2)}) %collective-permute-start.10) | collective-permute-done | bytes 524320 | tf_op jit(solution)/shard_map/ppermute | solution.py:24
  250.4 13.9 %collective-permute-done.11 = bf16[512,1024]{1,0:T(8,128)(2,1)S(1)} collective-permute-done((bf16[512,1024]{1,0:T(8,128)(2,1)S(1)}, bf16[512,1024]{1,0:T(8,128)(2,1)S(1)}, u32[]{:S(2)}, u32[]{:S(2)}) %collective-permute-start.11) | collective-permute-done | bytes 1048608 | tf_op jit(solution)/shard_map/ppermute | solution.py:24
  265.9 7.5 %fusion.9 = bf16[1,896,1024]{2,1,0:T(8,128)(2,1)S(1)} fusion(bf16[896,1024]{1,0:T(8,128)(2,1)} %copy-done.3, bf16[512,1024]{1,0:T(8,128)(2,1)} %get-tuple-element.4, bf16[512,1024]{1,0:T(8,128)(2,1)S(1)} %get-tuple-element.3), kind=kOutput, calls=%fused_computation.26 | convolution fusion | flops 4045537280 | bytes 5767168 | tf_op jit(solution)/shard_map/dot_general | solution.py:86
  273.4 4.8 %copy.9 = bf16[1,896,1024]{2,0,1:T(2,128)(2,1)} copy(bf16[1,896,1024]{2,1,0:T(8,128)(2,1)S(1)} %fusion.9) | data formatting | bytes 3670016 | tf_op jit(solution)/shard_map/broadcast_in_dim | solution.py:89
  278.7 11.4 %reduce = bf16[896,1024]{1,0:T(8,128)(2,1)S(1)} reduce(bf16[896,1,1024]{2,1,0:T(2,128)(2,1)} %bitcast.69, bf16[]{:T(256)} %broadcast.84), dimensions={1}, to_apply=%bitcast.68.reduce_sub_computation | reduce | bytes 3670018
  290.1 3.7 %reshape.106 = bf16[8,2,57344]{2,1,0:T(2,128)(2,1)} reshape(bf16[896,1024]{1,0:T(8,128)(2,1)S(1)} %reduce) | data formatting | bytes 3670016
  293.8 3.6 %all-to-all-start.1 = ((bf16[8,2,57344]{2,1,0:T(2,128)(2,1)}), bf16[8,2,57344]{2,1,0:T(2,128)(2,1)S(1)}, u32[]{:S(2)}, u32[]{:S(2)}) async-start(bf16[8,2,57344]{2,1,0:T(2,128)(2,1)} %reshape.106), calls=%async_computation.1 | async-start | bytes 3670016 | tf_op jit(solution)/shard_map/all_to_all | solution.py:89
  297.4 29.7 %all-to-all-done.1 = bf16[8,2,57344]{2,1,0:T(2,128)(2,1)S(1)} async-done(((bf16[8,2,57344]{2,1,0:T(2,128)(2,1)}), bf16[8,2,57344]{2,1,0:T(2,128)(2,1)S(1)}, u32[]{:S(2)}, u32[]{:S(2)}) %all-to-all-start.1) | async-done | bytes 1835040 | tf_op jit(solution)/shard_map/all_to_all | solution.py:89
  327.1 4.1 %reshape.107 = bf16[896,1,1024]{2,1,0:T(2,128)(2,1)} reshape(bf16[8,2,57344]{2,1,0:T(2,128)(2,1)S(1)} %all-to-all-done.1) | data formatting | bytes 3670016
  331.2 4.0 %copy.7 = bf16[1,896,1024]{2,1,0:T(8,128)(2,1)} copy(bf16[1,896,1024]{2,0,1:T(2,128)(2,1)} %bitcast.70) | data formatting | bytes 3670016
  335.2 2.2 gather_fusion.1
  (53 shorter events, 32.9 us)
Async XLA Ops:
  6.4 56.9 %all-to-all-start = ((bf16[8,112,1024]{2,1,0:T(8,128)(2,1)}), bf16[8,112,1024]{2,1,0:T(8,128)(2,1)S(1)}, u32[]{:S(2)}, u32[]{:S(2)}) async-start(bf16[8,112,1024]{2,1,0:T(8,128)(2,1)} %bitcast.71), calls=%async_computation | async-start | bytes 3670016 | tf_op jit(solution)/shard_map/all_to_all | solution.py:76
  63.7 2.4 copy-start.1
  66.1 1.3 copy-start
  67.5 24.5 %collective-permute-start = (bf16[512,1024]{1,0:T(8,128)(2,1)S(1)}, bf16[512,1024]{1,0:T(8,128)(2,1)S(1)}, u32[]{:S(2)}, u32[]{:S(2)}) collective-permute-start(bf16[512,1024]{1,0:T(8,128)(2,1)S(1)} %dynamic-slice_bitcast_fusion.2), channel_id=1, source_target_pairs={{0,1},{1,0},{2,3},{3,2},{4,5},{5,4},{6,7},{7,6},{8,9},{9,8},{10,11... | collective-permute-start | bytes 3145736 | tf_op jit(solution)/shard_map/ppermute | solution.py:24
  93.7 13.2 %collective-permute-start.1 = (bf16[256,1024]{1,0:T(8,128)(2,1)S(1)}, bf16[256,1024]{1,0:T(8,128)(2,1)S(1)}, u32[]{:S(2)}, u32[]{:S(2)}) collective-permute-start(bf16[256,1024]{1,0:T(8,128)(2,1)S(1)} %fusion.13), channel_id=1, source_target_pairs={{0,2},{1,3},{2,0},{3,1},{4,6},{5,7},{6,4},{7,5},{8,10},{9,11},{10,... | collective-permute-start | bytes 1572872 | tf_op jit(solution)/shard_map/ppermute | solution.py:24
  107.1 9.2 %collective-permute-start.2 = (bf16[256,1024]{1,0:T(8,128)(2,1)S(1)}, bf16[256,1024]{1,0:T(8,128)(2,1)S(1)}, u32[]{:S(2)}, u32[]{:S(2)}) collective-permute-start(bf16[256,1024]{1,0:T(8,128)(2,1)S(1)} %fusion.12), channel_id=1, source_target_pairs={{0,2},{1,3},{2,0},{3,1},{4,6},{5,7},{6,4},{7,5},{8,10},{9,11},{10,... | collective-permute-start | bytes 1572872 | tf_op jit(solution)/shard_map/ppermute | solution.py:24
  116.5 20.3 %collective-permute-start.3 = (bf16[512,1024]{1,0:T(8,128)(2,1)S(1)}, bf16[512,1024]{1,0:T(8,128)(2,1)S(1)}, u32[]{:S(2)}, u32[]{:S(2)}) collective-permute-start(bf16[512,1024]{1,0:T(8,128)(2,1)S(1)} %pad_maximum_fusion), channel_id=1, source_target_pairs={{0,1},{1,0},{2,3},{3,2},{4,5},{5,4},{6,7},{7,6},{8,9},{9,8},{10,11... | collective-permute-start | bytes 3145736 | tf_op jit(solution)/shard_map/ppermute | solution.py:24
  137.4 2.5 copy-start.2
  144.4 19.4 %collective-permute-start.4 = (bf16[512,1024]{1,0:T(8,128)(2,1)S(1)}, bf16[512,1024]{1,0:T(8,128)(2,1)S(1)}, u32[]{:S(2)}, u32[]{:S(2)}) collective-permute-start(bf16[512,1024]{1,0:T(8,128)(2,1)S(1)} %dynamic-slice_bitcast_fusion.1), channel_id=1, source_target_pairs={{0,1},{1,0},{2,3},{3,2},{4,5},{5,4},{6,7},{7,6},{8,9},{9,8},{10,11... | collective-permute-start | bytes 3145736 | tf_op jit(solution)/shard_map/ppermute | solution.py:24
  164.3 14.1 %collective-permute-start.5 = (bf16[256,1024]{1,0:T(8,128)(2,1)S(1)}, bf16[256,1024]{1,0:T(8,128)(2,1)S(1)}, u32[]{:S(2)}, u32[]{:S(2)}) collective-permute-start(bf16[256,1024]{1,0:T(8,128)(2,1)S(1)} %fusion.14), channel_id=1, source_target_pairs={{0,2},{1,3},{2,0},{3,1},{4,6},{5,7},{6,4},{7,5},{8,10},{9,11},{10,... | collective-permute-start | bytes 1572872 | tf_op jit(solution)/shard_map/ppermute | solution.py:24
  178.6 9.2 %collective-permute-start.6 = (bf16[256,1024]{1,0:T(8,128)(2,1)S(1)}, bf16[256,1024]{1,0:T(8,128)(2,1)S(1)}, u32[]{:S(2)}, u32[]{:S(2)}) collective-permute-start(bf16[256,1024]{1,0:T(8,128)(2,1)S(1)} %fusion.11), channel_id=1, source_target_pairs={{0,2},{1,3},{2,0},{3,1},{4,6},{5,7},{6,4},{7,5},{8,10},{9,11},{10,... | collective-permute-start | bytes 1572872 | tf_op jit(solution)/shard_map/ppermute | solution.py:24
  188.0 16.3 %collective-permute-start.7 = (bf16[512,1024]{1,0:T(8,128)(2,1)S(1)}, bf16[512,1024]{1,0:T(8,128)(2,1)S(1)}, u32[]{:S(2)}, u32[]{:S(2)}) collective-permute-start(bf16[512,1024]{1,0:T(8,128)(2,1)S(1)} %pad_maximum_fusion.1), channel_id=1, source_target_pairs={{0,1},{1,0},{2,3},{3,2},{4,5},{5,4},{6,7},{7,6},{8,9},{9,8},{10,11... | collective-permute-start | bytes 3145736 | tf_op jit(solution)/shard_map/ppermute | solution.py:24
  209.6 2.4 copy-start.3
  212.1 15.4 %collective-permute-start.8 = (bf16[512,1024]{1,0:T(8,128)(2,1)S(1)}, bf16[512,1024]{1,0:T(8,128)(2,1)S(1)}, u32[]{:S(2)}, u32[]{:S(2)}) collective-permute-start(bf16[512,1024]{1,0:T(8,128)(2,1)S(1)} %dynamic-slice_bitcast_fusion), channel_id=1, source_target_pairs={{0,1},{1,0},{2,3},{3,2},{4,5},{5,4},{6,7},{7,6},{8,9},{9,8},{10,11... | collective-permute-start | bytes 3145736 | tf_op jit(solution)/shard_map/ppermute | solution.py:24
  228.0 11.9 %collective-permute-start.9 = (bf16[256,1024]{1,0:T(8,128)(2,1)S(1)}, bf16[256,1024]{1,0:T(8,128)(2,1)S(1)}, u32[]{:S(2)}, u32[]{:S(2)}) collective-permute-start(bf16[256,1024]{1,0:T(8,128)(2,1)S(1)} %fusion.15), channel_id=1, source_target_pairs={{0,2},{1,3},{2,0},{3,1},{4,6},{5,7},{6,4},{7,5},{8,10},{9,11},{10,... | collective-permute-start | bytes 1572872 | tf_op jit(solution)/shard_map/ppermute | solution.py:24
  240.0 9.2 %collective-permute-start.10 = (bf16[256,1024]{1,0:T(8,128)(2,1)S(1)}, bf16[256,1024]{1,0:T(8,128)(2,1)S(1)}, u32[]{:S(2)}, u32[]{:S(2)}) collective-permute-start(bf16[256,1024]{1,0:T(8,128)(2,1)S(1)} %fusion.10), channel_id=1, source_target_pairs={{0,2},{1,3},{2,0},{3,1},{4,6},{5,7},{6,4},{7,5},{8,10},{9,11},{10,... | collective-permute-start | bytes 1572872 | tf_op jit(solution)/shard_map/ppermute | solution.py:24
  249.4 14.9 %collective-permute-start.11 = (bf16[512,1024]{1,0:T(8,128)(2,1)S(1)}, bf16[512,1024]{1,0:T(8,128)(2,1)S(1)}, u32[]{:S(2)}, u32[]{:S(2)}) collective-permute-start(bf16[512,1024]{1,0:T(8,128)(2,1)S(1)} %pad_maximum_fusion.2), channel_id=1, source_target_pairs={{0,1},{1,0},{2,3},{3,2},{4,5},{5,4},{6,7},{7,6},{8,9},{9,8},{10,11... | collective-permute-start | bytes 3145736 | tf_op jit(solution)/shard_map/ppermute | solution.py:24
  293.8 33.3 %all-to-all-start.1 = ((bf16[8,2,57344]{2,1,0:T(2,128)(2,1)}), bf16[8,2,57344]{2,1,0:T(2,128)(2,1)S(1)}, u32[]{:S(2)}, u32[]{:S(2)}) async-start(bf16[8,2,57344]{2,1,0:T(2,128)(2,1)} %reshape.106), calls=%async_computation.1 | async-start | bytes 3670016 | tf_op jit(solution)/shard_map/all_to_all | solution.py:89
where the time goes:
time: 341 us; the launch traced here: 340 us
  waiting for transfers between devices  185 us (54%)
  blocking collectives  43.7 us (13%)
  starting transfers between devices  33.2 us (10%)
  other arithmetic  24.9 us (7%)
  local copies, waits for them, and re-layouts  24.4 us (7%)
  matrix products  24 us (7%)
  between operations  4.74 us (1%)
    ppermute x12, waiting for transfers between devices, partner_2(): return lax.ppermute(value, axis, pairs)  155 us
    psum x1, blocking collectives, body(): totals = lax.psum(expert_sums, 'fsdp')  43.7 us
    all_to_all x1, waiting for transfers between devices, body(): lax.all_to_all(update[None], 'fsdp', split_axis=1, concat_axis=0, tiled=T...  29.7 us
    ppermute x12, starting transfers between devices, partner_2(): return lax.ppermute(value, axis, pairs)  22.3 us
    unnamed x12, local copies, waits for them, and re-layouts  13.6 us
    dot_general x3, matrix products, body(): jnp.dot(current, poly, preferred_element_type=jnp.float32)  11.7 us
    unnamed x1, other arithmetic  11.4 us
    all_to_all x1, starting transfers between devices, body(): lax.all_to_all(outbound, 'fsdp', split_axis=0, concat_axis=1, tiled=True)[0]  7.28 us
  transfers between devices with their start and end apart: 14, of which 13 were waited for; matrix products, arithmetic and copies ran while one was open for 1% of the time, Pallas kernels for 0%

commit v1 on v0

--- a/solution.py
+++ b/solution.py
@@ -68,7 +68,9 @@
         jnp.where(owner_row[None, :] == places[:, None], places[None, :], 0), axis=1
     ).astype(jnp.int32)
     expert_sums = jnp.sum(jnp.square(gradients.astype(jnp.float32)), axis=(1, 2))
-    totals = lax.psum(expert_sums, "fsdp")
+    totals = expert_sums
+    for hop in (1, 2, 4):
+        totals = totals + lax.ppermute(totals, "fsdp", [(dev, dev ^ hop) for dev in range(8)])
     own_expert = lax.dynamic_index_in_dim(inverse, fsdp_index // SHARE, 0, keepdims=False)
     square_sum = lax.dynamic_index_in_dim(totals, own_expert, 0, keepdims=False)
     ordered = jnp.take(gradients, inverse, axis=0)

time: 341 us -> 351 us (1.029)
  waiting for transfers between devices: 185 us -> 239 us
  blocking collectives: 43.7 us -> 0 us
    psum x1 -> x0, blocking collectives: 43.7 us -> none  [body(): totals = lax.psum(expert_sums, 'fsdp')]
    ppermute x0 -> x3, waiting for transfers between devices: none -> 30.8 us  [body(): lax.ppermute(totals, 'fsdp', [(dev, dev ^ hop) for dev in range(8)])]
    ppermute x12, waiting for transfers between devices: 155 us -> 175 us  [partner_2(): return lax.ppermute(value, axis, pairs)]
    ppermute x12, starting transfers between devices: 22.3 us -> 13.6 us  [partner_2(): return lax.ppermute(value, axis, pairs)]
    ppermute x0 -> x3, starting transfers between devices: none -> 7.25 us  [body(): lax.ppermute(totals, 'fsdp', [(dev, dev ^ hop) for dev in range(8)])]
  transfers between devices with their start and end apart: 14 -> 17, of which waited for: 13 -> 16; matrix products, arithmetic and copies ran while one was open for 1% -> 1% of each run, Pallas kernels for 0% -> 0%
where the time goes in v1:
time: 351 us
  waiting for transfers between devices  239 us (68%)
  starting transfers between devices  34.1 us (10%)
  other arithmetic  25.1 us (7%)
  local copies, waits for them, and re-layouts  24.4 us (7%)
  matrix products  23.8 us (7%)
  between operations  4.73 us (1%)
    ppermute x12, waiting for transfers between devices, partner_2(): return lax.ppermute(value, axis, pairs)  175 us
    all_to_all x1, waiting for transfers between devices, body(): lax.all_to_all(update[None], 'fsdp', split_axis=1, concat_axis=0, tiled=T...  32.4 us
    ppermute x3, waiting for transfers between devices, body(): lax.ppermute(totals, 'fsdp', [(dev, dev ^ hop) for dev in range(8)])  30.8 us
    unnamed x12, local copies, waits for them, and re-layouts  13.6 us
    ppermute x12, starting transfers between devices, partner_2(): return lax.ppermute(value, axis, pairs)  13.6 us
    dot_general x3, matrix products, body(): jnp.dot(current, poly, preferred_element_type=jnp.float32)  11.7 us
    unnamed x1, other arithmetic  11.4 us
    all_to_all x1, starting transfers between devices, body(): lax.all_to_all(outbound, 'fsdp', split_axis=0, concat_axis=1, tiled=True)[0]  7.28 us
  transfers between devices with their start and end apart: 17, of which 16 were waited for; matrix products, arithmetic and copies ran while one was open for 1% of the time, Pallas kernels for 0%

profile of v1, /device:TPU:0, one launch (start us, length us, event | category | flops | bytes accessed | tf_op | source)
XLA Modules:
  0.0 350.8 jit_solution(9008918139421885259)
XLA Ops:
  2.7 2.2 gather_fusion
  6.4 7.3 %all-to-all-start = ((bf16[8,112,1024]{2,1,0:T(8,128)(2,1)}), bf16[8,112,1024]{2,1,0:T(8,128)(2,1)S(1)}, u32[]{:S(2)}, u32[]{:S(2)}) async-start(bf16[8,112,1024]{2,1,0:T(8,128)(2,1)} %bitcast.71), calls=%async_computation | async-start | bytes 3670016 | tf_op jit(solution)/shard_map/all_to_all | solution.py:78
  20.3 8.4 %collective-permute-done = f32[2]{0:T(128)S(1)} collective-permute-done((f32[2]{0:T(128)S(1)}, f32[2]{0:T(128)S(1)}, u32[]{:S(2)}, u32[]{:S(2)}) %collective-permute-start) | collective-permute-done | bytes 40 | tf_op jit(solution)/shard_map/ppermute | solution.py:73
  30.4 14.1 %collective-permute-done.1 = f32[2]{0:T(128)S(1)} collective-permute-done((f32[2]{0:T(128)S(1)}, f32[2]{0:T(128)S(1)}, u32[]{:S(2)}, u32[]{:S(2)}) %collective-permute-start.1) | collective-permute-done | bytes 40 | tf_op jit(solution)/shard_map/ppermute | solution.py:73
  44.5 3.5 %collective-permute-start.2 = (f32[2]{0:T(128)S(1)}, f32[2]{0:T(128)S(1)}, u32[]{:S(2)}, u32[]{:S(2)}) collective-permute-start(f32[2]{0:T(128)S(1)} %add.96), channel_id=1, source_target_pairs={{0,4},{1,5},{2,6},{3,7},{4,0},{5,1},{6,2},{7,3},{8,12},{9,13},{10,... | collective-permute-start | bytes 32 | tf_op jit(solution)/shard_map/ppermute | solution.py:73
  48.0 8.4 %collective-permute-done.2 = f32[2]{0:T(128)S(1)} collective-permute-done((f32[2]{0:T(128)S(1)}, f32[2]{0:T(128)S(1)}, u32[]{:S(2)}, u32[]{:S(2)}) %collective-permute-start.2) | collective-permute-done | bytes 40 | tf_op jit(solution)/shard_map/ppermute | solution.py:73
  58.1 2.4 bitcast_convert_fusion
  63.5 22.4 %collective-permute-done.3 = bf16[512,1024]{1,0:T(8,128)(2,1)S(1)} collective-permute-done((bf16[512,1024]{1,0:T(8,128)(2,1)S(1)}, bf16[512,1024]{1,0:T(8,128)(2,1)S(1)}, u32[]{:S(2)}, u32[]{:S(2)}) %collective-permute-start.3) | collective-permute-done | bytes 1048608 | tf_op jit(solution)/shard_map/ppermute | solution.py:24
  88.3 11.2 %collective-permute-done.4 = bf16[256,1024]{1,0:T(8,128)(2,1)S(1)} collective-permute-done((bf16[256,1024]{1,0:T(8,128)(2,1)S(1)}, bf16[256,1024]{1,0:T(8,128)(2,1)S(1)}, u32[]{:S(2)}, u32[]{:S(2)}) %collective-permute-start.4) | collective-permute-done | bytes 524320 | tf_op jit(solution)/shard_map/ppermute | solution.py:24
  101.5 10.4 %collective-permute-done.5 = bf16[256,1024]{1,0:T(8,128)(2,1)S(1)} collective-permute-done((bf16[256,1024]{1,0:T(8,128)(2,1)S(1)}, bf16[256,1024]{1,0:T(8,128)(2,1)S(1)}, u32[]{:S(2)}, u32[]{:S(2)}) %collective-permute-start.5) | collective-permute-done | bytes 524320 | tf_op jit(solution)/shard_map/ppermute | solution.py:24
  112.9 21.7 %collective-permute-done.6 = bf16[512,1024]{1,0:T(8,128)(2,1)S(1)} collective-permute-done((bf16[512,1024]{1,0:T(8,128)(2,1)S(1)}, bf16[512,1024]{1,0:T(8,128)(2,1)S(1)}, u32[]{:S(2)}, u32[]{:S(2)}) %collective-permute-start.6) | collective-permute-done | bytes 1048608 | tf_op jit(solution)/shard_map/ppermute | solution.py:24
  135.2 2.5 add_convert_fusion.2
  139.7 2.4 convolution_convert_fusion.1
  142.6 21.4 %collective-permute-done.7 = bf16[512,1024]{1,0:T(8,128)(2,1)S(1)} collective-permute-done((bf16[512,1024]{1,0:T(8,128)(2,1)S(1)}, bf16[512,1024]{1,0:T(8,128)(2,1)S(1)}, u32[]{:S(2)}, u32[]{:S(2)}) %collective-permute-start.7) | collective-permute-done | bytes 1048608 | tf_op jit(solution)/shard_map/ppermute | solution.py:24
  166.2 10.1 %collective-permute-done.8 = bf16[256,1024]{1,0:T(8,128)(2,1)S(1)} collective-permute-done((bf16[256,1024]{1,0:T(8,128)(2,1)S(1)}, bf16[256,1024]{1,0:T(8,128)(2,1)S(1)}, u32[]{:S(2)}, u32[]{:S(2)}) %collective-permute-start.8) | collective-permute-done | bytes 524320 | tf_op jit(solution)/shard_map/ppermute | solution.py:24
  178.3 7.4 %collective-permute-done.9 = bf16[256,1024]{1,0:T(8,128)(2,1)S(1)} collective-permute-done((bf16[256,1024]{1,0:T(8,128)(2,1)S(1)}, bf16[256,1024]{1,0:T(8,128)(2,1)S(1)}, u32[]{:S(2)}, u32[]{:S(2)}) %collective-permute-start.9) | collective-permute-done | bytes 524320 | tf_op jit(solution)/shard_map/ppermute | solution.py:24
  186.3 18.5 %collective-permute-done.10 = bf16[512,1024]{1,0:T(8,128)(2,1)S(1)} collective-permute-done((bf16[512,1024]{1,0:T(8,128)(2,1)S(1)}, bf16[512,1024]{1,0:T(8,128)(2,1)S(1)}, u32[]{:S(2)}, u32[]{:S(2)}) %collective-permute-start.10) | collective-permute-done | bytes 1048608 | tf_op jit(solution)/shard_map/ppermute | solution.py:24
  205.5 2.5 add_convert_fusion.1
  210.1 2.4 convolution_convert_fusion
  212.9 17.6 %collective-permute-done.11 = bf16[512,1024]{1,0:T(8,128)(2,1)S(1)} collective-permute-done((bf16[512,1024]{1,0:T(8,128)(2,1)S(1)}, bf16[512,1024]{1,0:T(8,128)(2,1)S(1)}, u32[]{:S(2)}, u32[]{:S(2)}) %collective-permute-start.11) | collective-permute-done | bytes 1048608 | tf_op jit(solution)/shard_map/ppermute | solution.py:24
  232.9 12.4 %collective-permute-done.12 = bf16[256,1024]{1,0:T(8,128)(2,1)S(1)} collective-permute-done((bf16[256,1024]{1,0:T(8,128)(2,1)S(1)}, bf16[256,1024]{1,0:T(8,128)(2,1)S(1)}, u32[]{:S(2)}, u32[]{:S(2)}) %collective-permute-start.12) | collective-permute-done | bytes 524320 | tf_op jit(solution)/shard_map/ppermute | solution.py:24
  247.2 7.4 %collective-permute-done.13 = bf16[256,1024]{1,0:T(8,128)(2,1)S(1)} collective-permute-done((bf16[256,1024]{1,0:T(8,128)(2,1)S(1)}, bf16[256,1024]{1,0:T(8,128)(2,1)S(1)}, u32[]{:S(2)}, u32[]{:S(2)}) %collective-permute-start.13) | collective-permute-done | bytes 524320 | tf_op jit(solution)/shard_map/ppermute | solution.py:24
  255.2 14.8 %collective-permute-done.14 = bf16[512,1024]{1,0:T(8,128)(2,1)S(1)} collective-permute-done((bf16[512,1024]{1,0:T(8,128)(2,1)S(1)}, bf16[512,1024]{1,0:T(8,128)(2,1)S(1)}, u32[]{:S(2)}, u32[]{:S(2)}) %collective-permute-start.14) | collective-permute-done | bytes 1048608 | tf_op jit(solution)/shard_map/ppermute | solution.py:24
  271.5 7.6 %fusion.9 = bf16[1,896,1024]{2,1,0:T(8,128)(2,1)S(1)} fusion(bf16[896,1024]{1,0:T(8,128)(2,1)} %copy-done.3, bf16[512,1024]{1,0:T(8,128)(2,1)} %get-tuple-element.4, bf16[512,1024]{1,0:T(8,128)(2,1)S(1)} %get-tuple-element.3), kind=kOutput, calls=%fused_computation.26 | convolution fusion | flops 4045537280 | bytes 5767168 | tf_op jit(solution)/shard_map/dot_general | solution.py:88
  279.1 4.8 %copy.9 = bf16[1,896,1024]{2,0,1:T(2,128)(2,1)} copy(bf16[1,896,1024]{2,1,0:T(8,128)(2,1)S(1)} %fusion.9) | data formatting | bytes 3670016 | tf_op jit(solution)/shard_map/broadcast_in_dim | solution.py:91
  284.5 11.4 %reduce = bf16[896,1024]{1,0:T(8,128)(2,1)S(1)} reduce(bf16[896,1,1024]{2,1,0:T(2,128)(2,1)} %bitcast.69, bf16[]{:T(256)} %broadcast.84), dimensions={1}, to_apply=%bitcast.68.reduce_sub_computation | reduce | bytes 3670018
  295.9 3.7 %reshape.106 = bf16[8,2,57344]{2,1,0:T(2,128)(2,1)} reshape(bf16[896,1024]{1,0:T(8,128)(2,1)S(1)} %reduce) | data formatting | bytes 3670016
  299.5 6.0 %all-to-all-start.1 = ((bf16[8,2,57344]{2,1,0:T(2,128)(2,1)}), bf16[8,2,57344]{2,1,0:T(2,128)(2,1)S(1)}, u32[]{:S(2)}, u32[]{:S(2)}) async-start(bf16[8,2,57344]{2,1,0:T(2,128)(2,1)} %reshape.106), calls=%async_computation.1 | async-start | bytes 3670016 | tf_op jit(solution)/shard_map/all_to_all | solution.py:91
  305.5 32.4 %all-to-all-done.1 = bf16[8,2,57344]{2,1,0:T(2,128)(2,1)S(1)} async-done(((bf16[8,2,57344]{2,1,0:T(2,128)(2,1)}), bf16[8,2,57344]{2,1,0:T(2,128)(2,1)S(1)}, u32[]{:S(2)}, u32[]{:S(2)}) %all-to-all-start.1) | async-done | bytes 1835040 | tf_op jit(solution)/shard_map/all_to_all | solution.py:91
  337.9 4.1 %reshape.107 = bf16[896,1,1024]{2,1,0:T(2,128)(2,1)} reshape(bf16[8,2,57344]{2,1,0:T(2,128)(2,1)S(1)} %all-to-all-done.1) | data formatting | bytes 3670016
  342.0 4.0 %copy.7 = bf16[1,896,1024]{2,1,0:T(8,128)(2,1)} copy(bf16[1,896,1024]{2,0,1:T(2,128)(2,1)} %bitcast.70) | data formatting | bytes 3670016
  346.0 2.2 gather_fusion.1
  (61 shorter events, 38.7 us)
Async XLA Ops:
  6.4 51.3 %all-to-all-start = ((bf16[8,112,1024]{2,1,0:T(8,128)(2,1)}), bf16[8,112,1024]{2,1,0:T(8,128)(2,1)S(1)}, u32[]{:S(2)}, u32[]{:S(2)}) async-start(bf16[8,112,1024]{2,1,0:T(8,128)(2,1)} %bitcast.71), calls=%async_computation | async-start | bytes 3670016 | tf_op jit(solution)/shard_map/all_to_all | solution.py:78
  15.7 13.0 %collective-permute-start = (f32[2]{0:T(128)S(1)}, f32[2]{0:T(128)S(1)}, u32[]{:S(2)}, u32[]{:S(2)}) collective-permute-start(f32[2]{0:T(128)S(1)} %multiply_reduce_fusion), channel_id=1, source_target_pairs={{0,1},{1,0},{2,3},{3,2},{4,5},{5,4},{6,7},{7,6},{8,9},{9,8},{10,11... | collective-permute-start | bytes 32 | tf_op jit(solution)/shard_map/ppermute | solution.py:73
  28.7 15.8 %collective-permute-start.1 = (f32[2]{0:T(128)S(1)}, f32[2]{0:T(128)S(1)}, u32[]{:S(2)}, u32[]{:S(2)}) collective-permute-start(f32[2]{0:T(128)S(1)} %add.95), channel_id=1, source_target_pairs={{0,2},{1,3},{2,0},{3,1},{4,6},{5,7},{6,4},{7,5},{8,10},{9,11},{10,... | collective-permute-start | bytes 32 | tf_op jit(solution)/shard_map/ppermute | solution.py:73
  44.5 11.9 %collective-permute-start.2 = (f32[2]{0:T(128)S(1)}, f32[2]{0:T(128)S(1)}, u32[]{:S(2)}, u32[]{:S(2)}) collective-permute-start(f32[2]{0:T(128)S(1)} %add.96), channel_id=1, source_target_pairs={{0,4},{1,5},{2,6},{3,7},{4,0},{5,1},{6,2},{7,3},{8,12},{9,13},{10,... | collective-permute-start | bytes 32 | tf_op jit(solution)/shard_map/ppermute | solution.py:73
  58.1 2.4 copy-start.1
  60.5 1.3 copy-start
  61.9 23.9 %collective-permute-start.3 = (bf16[512,1024]{1,0:T(8,128)(2,1)S(1)}, bf16[512,1024]{1,0:T(8,128)(2,1)S(1)}, u32[]{:S(2)}, u32[]{:S(2)}) collective-permute-start(bf16[512,1024]{1,0:T(8,128)(2,1)S(1)} %dynamic-slice_bitcast_fusion.2), channel_id=1, source_target_pairs={{0,1},{1,0},{2,3},{3,2},{4,5},{5,4},{6,7},{7,6},{8,9},{9,8},{10,11... | collective-permute-start | bytes 3145736 | tf_op jit(solution)/shard_map/ppermute | solution.py:24
  87.5 12.0 %collective-permute-start.4 = (bf16[256,1024]{1,0:T(8,128)(2,1)S(1)}, bf16[256,1024]{1,0:T(8,128)(2,1)S(1)}, u32[]{:S(2)}, u32[]{:S(2)}) collective-permute-start(bf16[256,1024]{1,0:T(8,128)(2,1)S(1)} %fusion.13), channel_id=1, source_target_pairs={{0,2},{1,3},{2,0},{3,1},{4,6},{5,7},{6,4},{7,5},{8,10},{9,11},{10,... | collective-permute-start | bytes 1572872 | tf_op jit(solution)/shard_map/ppermute | solution.py:24
  99.7 12.2 %collective-permute-start.5 = (bf16[256,1024]{1,0:T(8,128)(2,1)S(1)}, bf16[256,1024]{1,0:T(8,128)(2,1)S(1)}, u32[]{:S(2)}, u32[]{:S(2)}) collective-permute-start(bf16[256,1024]{1,0:T(8,128)(2,1)S(1)} %fusion.12), channel_id=1, source_target_pairs={{0,2},{1,3},{2,0},{3,1},{4,6},{5,7},{6,4},{7,5},{8,10},{9,11},{10,... | collective-permute-start | bytes 1572872 | tf_op jit(solution)/shard_map/ppermute | solution.py:24
  112.1 22.6 %collective-permute-start.6 = (bf16[512,1024]{1,0:T(8,128)(2,1)S(1)}, bf16[512,1024]{1,0:T(8,128)(2,1)S(1)}, u32[]{:S(2)}, u32[]{:S(2)}) collective-permute-start(bf16[512,1024]{1,0:T(8,128)(2,1)S(1)} %pad_maximum_fusion), channel_id=1, source_target_pairs={{0,1},{1,0},{2,3},{3,2},{4,5},{5,4},{6,7},{7,6},{8,9},{9,8},{10,11... | collective-permute-start | bytes 3145736 | tf_op jit(solution)/shard_map/ppermute | solution.py:24
  135.2 2.5 copy-start.2
  142.2 21.7 %collective-permute-start.7 = (bf16[512,1024]{1,0:T(8,128)(2,1)S(1)}, bf16[512,1024]{1,0:T(8,128)(2,1)S(1)}, u32[]{:S(2)}, u32[]{:S(2)}) collective-permute-start(bf16[512,1024]{1,0:T(8,128)(2,1)S(1)} %dynamic-slice_bitcast_fusion.1), channel_id=1, source_target_pairs={{0,1},{1,0},{2,3},{3,2},{4,5},{5,4},{6,7},{7,6},{8,9},{9,8},{10,11... | collective-permute-start | bytes 3145736 | tf_op jit(solution)/shard_map/ppermute | solution.py:24
  164.4 11.9 %collective-permute-start.8 = (bf16[256,1024]{1,0:T(8,128)(2,1)S(1)}, bf16[256,1024]{1,0:T(8,128)(2,1)S(1)}, u32[]{:S(2)}, u32[]{:S(2)}) collective-permute-start(bf16[256,1024]{1,0:T(8,128)(2,1)S(1)} %fusion.14), channel_id=1, source_target_pairs={{0,2},{1,3},{2,0},{3,1},{4,6},{5,7},{6,4},{7,5},{8,10},{9,11},{10,... | collective-permute-start | bytes 1572872 | tf_op jit(solution)/shard_map/ppermute | solution.py:24
  176.5 9.2 %collective-permute-start.9 = (bf16[256,1024]{1,0:T(8,128)(2,1)S(1)}, bf16[256,1024]{1,0:T(8,128)(2,1)S(1)}, u32[]{:S(2)}, u32[]{:S(2)}) collective-permute-start(bf16[256,1024]{1,0:T(8,128)(2,1)S(1)} %fusion.11), channel_id=1, source_target_pairs={{0,2},{1,3},{2,0},{3,1},{4,6},{5,7},{6,4},{7,5},{8,10},{9,11},{10,... | collective-permute-start | bytes 1572872 | tf_op jit(solution)/shard_map/ppermute | solution.py:24
  185.9 18.9 %collective-permute-start.10 = (bf16[512,1024]{1,0:T(8,128)(2,1)S(1)}, bf16[512,1024]{1,0:T(8,128)(2,1)S(1)}, u32[]{:S(2)}, u32[]{:S(2)}) collective-permute-start(bf16[512,1024]{1,0:T(8,128)(2,1)S(1)} %pad_maximum_fusion.1), channel_id=1, source_target_pairs={{0,1},{1,0},{2,3},{3,2},{4,5},{5,4},{6,7},{7,6},{8,9},{9,8},{10,11... | collective-permute-start | bytes 3145736 | tf_op jit(solution)/shard_map/ppermute | solution.py:24
  210.1 2.4 copy-start.3
  212.6 18.0 %collective-permute-start.11 = (bf16[512,1024]{1,0:T(8,128)(2,1)S(1)}, bf16[512,1024]{1,0:T(8,128)(2,1)S(1)}, u32[]{:S(2)}, u32[]{:S(2)}) collective-permute-start(bf16[512,1024]{1,0:T(8,128)(2,1)S(1)} %dynamic-slice_bitcast_fusion), channel_id=1, source_target_pairs={{0,1},{1,0},{2,3},{3,2},{4,5},{5,4},{6,7},{7,6},{8,9},{9,8},{10,11... | collective-permute-start | bytes 3145736 | tf_op jit(solution)/shard_map/ppermute | solution.py:24
  231.1 14.2 %collective-permute-start.12 = (bf16[256,1024]{1,0:T(8,128)(2,1)S(1)}, bf16[256,1024]{1,0:T(8,128)(2,1)S(1)}, u32[]{:S(2)}, u32[]{:S(2)}) collective-permute-start(bf16[256,1024]{1,0:T(8,128)(2,1)S(1)} %fusion.15), channel_id=1, source_target_pairs={{0,2},{1,3},{2,0},{3,1},{4,6},{5,7},{6,4},{7,5},{8,10},{9,11},{10,... | collective-permute-start | bytes 1572872 | tf_op jit(solution)/shard_map/ppermute | solution.py:24
  245.4 9.2 %collective-permute-start.13 = (bf16[256,1024]{1,0:T(8,128)(2,1)S(1)}, bf16[256,1024]{1,0:T(8,128)(2,1)S(1)}, u32[]{:S(2)}, u32[]{:S(2)}) collective-permute-start(bf16[256,1024]{1,0:T(8,128)(2,1)S(1)} %fusion.10), channel_id=1, source_target_pairs={{0,2},{1,3},{2,0},{3,1},{4,6},{5,7},{6,4},{7,5},{8,10},{9,11},{10,... | collective-permute-start | bytes 1572872 | tf_op jit(solution)/shard_map/ppermute | solution.py:24
  254.8 15.1 %collective-permute-start.14 = (bf16[512,1024]{1,0:T(8,128)(2,1)S(1)}, bf16[512,1024]{1,0:T(8,128)(2,1)S(1)}, u32[]{:S(2)}, u32[]{:S(2)}) collective-permute-start(bf16[512,1024]{1,0:T(8,128)(2,1)S(1)} %pad_maximum_fusion.2), channel_id=1, source_target_pairs={{0,1},{1,0},{2,3},{3,2},{4,5},{5,4},{6,7},{7,6},{8,9},{9,8},{10,11... | collective-permute-start | bytes 3145736 | tf_op jit(solution)/shard_map/ppermute | solution.py:24
  299.5 38.4 %all-to-all-start.1 = ((bf16[8,2,57344]{2,1,0:T(2,128)(2,1)}), bf16[8,2,57344]{2,1,0:T(2,128)(2,1)S(1)}, u32[]{:S(2)}, u32[]{:S(2)}) async-start(bf16[8,2,57344]{2,1,0:T(2,128)(2,1)} %reshape.106), calls=%async_computation.1 | async-start | bytes 3670016 | tf_op jit(solution)/shard_map/all_to_all | solution.py:91
